TPU v7x, 64 devices: a 2x2x8 block of a 4x4x8 slice. The times are simulated.
64 devices in a mesh: dp: 8 (over x, y, core), tp: 8 (over z).
Axes of the slice: x: 2, y: 2, z: 8, core: 2. Of those that a mesh axis runs over, the one named last changes fastest.
The devices are a block of a 4x4x8 slice.
Arguments:
- x: bfloat16 [16384, 3072], P('dp'), parts along dimension 0
- dy: bfloat16 [16384, 3072], P('dp'), parts along dimension 0
- gate: bfloat16 [16384, 8192], P('dp', 'tp'), parts along dimension 0
- up: bfloat16 [16384, 8192], P('dp', 'tp'), parts along dimension 0
- w_gate: bfloat16 [3072, 8192], P(None, 'tp')
- w_up: bfloat16 [3072, 8192], P(None, 'tp')
- w_down: bfloat16 [8192, 3072], P('tp')
Outputs:
- output 1: bfloat16 [16384, 3072], P('dp'), parts along dimension 0
- output 2: bfloat16 [24576, 8192], P('dp', 'tp'), parts along dimension 0
- output 3: bfloat16 [24576, 8192], P('dp', 'tp'), parts along dimension 0
- output 4: bfloat16 [65536, 3072], P(('dp', 'tp')), parts along dimension 0
There are 8 independent parts. A program takes and returns all parts, laid end to end along the dimension named above; an argument that names none is the same for every part.
All inputs are finite; a program needn't handle non-finite values.
Results may differ from a plain program's by a relative error of at most 0.012.
Values are sent between devices in bfloat16 or wider.
A program may use at most 768 MiB of HBM per device.

v0:
```python
import jax
import jax.numpy as jnp
from jax import lax
from jax.sharding import PartitionSpec as P


def act(gate, up):
    return jax.nn.silu(gate) * up


def solution(mesh):
    def step(x, dy, gate, up, w_gate, w_up, w_down):
        hidden, back = jax.vjp(act, gate.astype(jnp.float32), up.astype(jnp.float32))
        d_hidden = jnp.dot(dy, w_down.T, preferred_element_type=jnp.float32)
        d_gate, d_up = (g.astype(jnp.bfloat16) for g in back(d_hidden))
        term = jnp.dot(d_gate, w_gate.T, preferred_element_type=jnp.float32) + jnp.dot(d_up, w_up.T, preferred_element_type=jnp.float32)
        dx = lax.psum(term.astype(jnp.bfloat16), "tp")
        dw_gate = jnp.dot(x.T, d_gate, preferred_element_type=jnp.float32)
        dw_up = jnp.dot(x.T, d_up, preferred_element_type=jnp.float32)
        dw_down = jnp.dot(hidden.astype(jnp.bfloat16).T, dy, preferred_element_type=jnp.float32)
        return dx, *(g.astype(jnp.bfloat16) for g in (dw_gate, dw_up, dw_down))

    tokens, columns, rows = P("dp", None), P(None, "tp"), P("tp", None)
    return jax.shard_map(
        step,
        mesh=mesh,
        in_specs=(tokens, tokens, P("dp", "tp"), P("dp", "tp"), columns, columns, rows),
        out_specs=(tokens, P("dp", "tp"), P("dp", "tp"), P(("dp", "tp"), None)),
        check_vma=False,
    )
```

profile of v0, /device:TPU:21, one launch (start us, length us, event | category | flops | bytes accessed | tf_op | source)
XLA Modules:
  0.0 360.0 jit_solution(1609465817091103786)
XLA Ops:
  7.2 0.1 all-reduce.2.cloned.1.call-start
  7.2 24.7 %fusion.6 = (bf16[2048,1024]{1,0:T(8,128)(2,1)}, f32[2048,1024]{1,0:T(8,128)}) fusion(bf16[2048,1024]{1,0:T(8,128)(2,1)} %param.9, bf16[2048,1024]{1,0:T(8,128)(2,1)} %param.10, bf16[2048,3072]{1,0:T(8,128)(2,1)} %param.8, bf16[1024,3072]{1,0:T(8,128)(2,1)} %param.13), kind=kOutput, calls=%fused_computation.13 | convolution fusion | flops 12912164864 | bytes 39845888 | tf_op jit(solution)/shard_map/dot_general | solution.py:14
  32.0 19.8 %fusion.9 = f32[2048,3072]{1,0:T(8,128)} fusion(bf16[2048,1024]{1,0:T(8,128)(2,1)} %get-tuple-element.8, bf16[3072,1024]{1,0:T(8,128)(2,1)} %param.11), kind=kOutput, calls=%fused_computation.19 | convolution fusion | flops 12884901888 | bytes 35651584 | tf_op jit(solution)/shard_map/dot_general | solution.py:16
  51.8 25.9 %add_convert_fusion = bf16[2048,3072]{1,0:T(8,128)(2,1)} fusion(f32[2048,3072]{1,0:T(8,128)} %fusion.9, bf16[3072,1024]{1,0:T(8,128)(2,1)} %param.12, f32[2048,1024]{1,0:T(8,128)} %get-tuple-element.9, bf16[2048,1024]{1,0:T(8,128)(2,1)} %param.9), kind=kOutput, calls=%fused_computation | convolution fusion | flops 12912164864 | bytes 56623104 | tf_op jit(solution)/shard_map/dot_general | solution.py:16
  77.7 0.1 all-reduce.2.cloned.1.call-update
  77.8 18.6 %convert_bitcast_fusion.1 = bf16[3072,1024]{0,1:T(8,128)(2,1)} fusion(bf16[2048,1024]{1,0:T(8,128)(2,1)} %get-tuple-element.8, bf16[2048,3072]{1,0:T(8,128)(2,1)} %param.7), kind=kOutput, calls=%fused_computation.16 | convolution fusion | flops 12888047616 | bytes 23068672 | tf_op jit(solution)/shard_map/dot_general | solution.py:18
  96.4 8.6 %copy.11 = bf16[3072,1024]{1,0:T(8,128)(2,1)} copy(bf16[3072,1024]{0,1:T(8,128)(2,1)} %convert_bitcast_fusion.1) | data formatting | bytes 12582912
  105.0 22.4 %convert_bitcast_fusion = bf16[3072,1024]{0,1:T(8,128)(2,1)} fusion(bf16[2048,3072]{1,0:T(8,128)(2,1)} %param.7, f32[2048,1024]{1,0:T(8,128)} %get-tuple-element.9, bf16[2048,1024]{1,0:T(8,128)(2,1)} %param.9), kind=kOutput, calls=%fused_computation.15 | convolution fusion | flops 12902727680 | bytes 31457280 | tf_op jit(solution)/shard_map/dot_general | solution.py:19
  127.5 8.6 %copy.12 = bf16[3072,1024]{1,0:T(8,128)(2,1)} copy(bf16[3072,1024]{0,1:T(8,128)(2,1)} %convert_bitcast_fusion) | data formatting | bytes 12582912
  136.1 22.0 %convolution_convert_fusion = bf16[1024,3072]{1,0:T(8,128)(2,1)} fusion(bf16[2048,3072]{1,0:T(8,128)(2,1)} %param.8, bf16[2048,1024]{1,0:T(8,128)(2,1)} %param.10, bf16[2048,1024]{1,0:T(8,128)(2,1)} %param.9), kind=kOutput, calls=%fused_computation.17 | convolution fusion | flops 12904824832 | bytes 27262976 | tf_op jit(solution)/shard_map/dot_general | solution.py:20
  158.1 184.5 %all-reduce.2.cloned.1.call-done = bf16[2048,3072]{1,0:T(8,128)(2,1)} async-done(((bf16[2048,3072]{1,0:T(8,128)(2,1)}), bf16[2048,3072]{1,0:T(8,128)(2,1)}) %all-reduce.2.cloned.1.call-update) | async-done | bytes 12582928 | tf_op jit(solution)/shard_map/psum | solution.py:17
  342.6 10.5 %copy.14 = bf16[2048,3072]{1,0:T(8,128)(2,1)} copy(bf16[2048,3072]{1,0:T(8,128)(2,1)} %all-reduce.2.cloned.1.call-done) | data formatting | bytes 25165824
Async XLA Ops:
  7.2 335.4 %all-reduce.2.cloned.1.call-start = ((), (), s32[]{:S(2)}) async-start(), calls=%async_computation | async-start | bytes 25165824 | tf_op jit(solution)/shard_map/psum | solution.py:17
Sparse Core Ops, SparseCore 0:
  77.9 264.6 all-reduce.1
where the time goes:
time: 360 us
  waiting for transfers between devices  185 us (51%)
  matrix products  134 us (37%)
  local copies, waits for them, and re-layouts  27.8 us (8%)
  between operations  14.1 us (4%)
    psum x1, waiting for transfers between devices, step(): dx = lax.psum(term.astype(jnp.bfloat16), 'tp')  184 us
    unnamed x3, local copies, waits for them, and re-layouts  27.8 us
    dot_general x1, matrix products, step(): jnp.dot(d_up, w_up.T, preferred_element_type=jnp.float32)  25.9 us
    dot_general x1, matrix products, step(): d_hidden = jnp.dot(dy, w_down.T, preferred_element_type=jnp.float32)  24.7 us
    dot_general x1, matrix products, step(): dw_up = jnp.dot(x.T, d_up, preferred_element_type=jnp.float32)  22.4 us
    dot_general x1, matrix products, step(): jnp.dot(hidden.astype(jnp.bfloat16).T, dy, preferred_element_type=jnp.flo...  22 us
    dot_general x1, matrix products, step(): jnp.dot(d_gate, w_gate.T, preferred_element_type=jnp.float32)  19.8 us
    dot_general x1, matrix products, step(): dw_gate = jnp.dot(x.T, d_gate, preferred_element_type=jnp.float32)  18.6 us
  transfers between devices with their start and end apart: 1, of which 1 were waited for; matrix products, arithmetic and copies ran while one was open for 22% of the time, Pallas kernels for 0%

commit v1 on v0

v1 whole, which is shorter than its diff:
```python
import functools
import jax
import jax.numpy as jnp
from jax import lax
from jax.experimental import pallas as pl
from jax.experimental.pallas import tpu as pltpu
from jax.sharding import PartitionSpec as P


MESH = pl.DeviceIdType.MESH
F32, BF16 = jnp.float32, jnp.bfloat16
NT = (((1,), (1,)), ((), ()))
TN = (((0,), (0,)), ((), ()))


def rs_kernel(n, dy, gate, up, wd, wg, wu, dg_o, du_o, hid_o, *rest):
    outs, (wd_v, wg_v, wu_v, dy_v, g_v, u_v, dg_v, du_v, h_v, term, slots,
           w_sem, in_sem, d_sem, send_sem, recv_sem, o_sem) = rest[:4], rest[4:]
    me = lax.axis_index("tp")
    sides = (lax.rem(me + 1, n), lax.rem(me + n - 1, n))
    half = dy_v.shape[0] // 2
    cols = slots.shape[3]
    ff, width = wd_v.shape
    fb = 256
    nb = 512
    wp = cols // nb

    def row0(s, d):
        chunk = lax.rem(me + n - 1 - s, n) if d == 0 else lax.rem(me + 1 + s, n)
        return pl.multiple_of(chunk * (2 * half) + d * half, half)

    def inputs(s):
        copies = []
        for d in range(2):
            src, dst = pl.ds(row0(s, d), half), pl.ds(d * half, half)
            for i, (a, v) in enumerate(((dy, dy_v), (gate, g_v), (up, u_v))):
                copies.append(pltpu.make_async_copy(a.at[src], v.at[dst], in_sem.at[d, i]))
        return copies

    def w_down_copy(i):
        at = pl.ds(i * fb, fb)
        return pltpu.make_async_copy(wd.at[at], wd_v.at[at], w_sem.at[0, i])

    def w_in_copies(i):
        at = pl.ds(i * nb, nb)
        return [pltpu.make_async_copy(a.at[at], v.at[at], w_sem.at[1 + k, i]) for k, (a, v) in enumerate(((wg, wg_v), (wu, wu_v)))]

    def d_copies(s):
        copies = []
        for d in range(2):
            src, dst = pl.ds(d * half, half), pl.ds(row0(s, d), half)
            for i, (v, a) in enumerate(((dg_v, dg_o), (du_v, du_o), (h_v, hid_o))):
                copies.append(pltpu.make_async_copy(v.at[src], a.at[dst], d_sem.at[d, i]))
        return copies

    for c in inputs(0):
        c.start()
    for i in range(ff // fb):
        w_down_copy(i).start()
    for i in range(width // nb):
        for c in w_in_copies(i):
            c.start()

    barrier = pltpu.get_barrier_semaphore()
    for side in sides:
        pl.semaphore_signal(barrier, inc=1, device_id={"tp": side}, device_id_type=MESH)
    pl.semaphore_wait(barrier, 2)

    def gradients(s, first):
        for c in inputs(s):
            c.wait()
        if not first:
            for c in d_copies(s):
                c.wait()

        def block(i, _):
            if first:
                w_down_copy(i).wait()
            at = pl.ds(pl.multiple_of(i * fb, fb), fb)
            dh = lax.dot_general(dy_v[...], wd_v[at, :], NT, preferred_element_type=F32)
            g, u = g_v[:, at].astype(F32), u_v[:, at].astype(F32)
            sig = jax.nn.sigmoid(g)
            silu = g * sig
            h_v[:, at] = (silu * u).astype(BF16)
            du_v[:, at] = (dh * silu).astype(BF16)
            dg_v[:, at] = (dh * u * (sig + silu * (1.0 - sig))).astype(BF16)
            return 0

        lax.fori_loop(0, ff // fb, block, 0)
        for c in d_copies(s):
            c.start()

    def product(h, first):
        def block(i, _):
            if first is not None:
                @pl.when(first)
                def _():
                    for c in w_in_copies(h * wp + i):
                        c.wait()
            at = pl.ds(pl.multiple_of(h * cols + i * nb, nb), nb)
            t = lax.dot_general(dg_v[...], wg_v[at, :], NT, preferred_element_type=F32)
            t += lax.dot_general(du_v[...], wu_v[at, :], NT, preferred_element_type=F32)
            term[h, :, pl.ds(pl.multiple_of(i * nb, nb), nb)] = t
            return 0

        lax.fori_loop(0, wp, block, 0)

    def send(s, d, h):
        k = 2 * h + d
        return pltpu.make_async_remote_copy(
            src_ref=slots.at[lax.rem(s + n - 1, n), k],
            dst_ref=slots.at[s, k],
            send_sem=send_sem.at[s, k],
            recv_sem=recv_sem.at[s, k],
            device_id={"tp": sides[d]},
            device_id_type=MESH,
        )

    def results(h):
        copies = []
        for d in range(2):
            for q in range(2):
                r = half // 2
                copies.append(pltpu.make_async_copy(
                    slots.at[n - 2, 2 * h + d, pl.ds(q * r, r)],
                    outs[2 * d + q].at[:, pl.ds(h * cols, cols)], o_sem.at[h, d, q]))
        return copies

    def stream(s, h):
        for d in range(2):
            k = 2 * h + d
            at = pl.ds(d * half, half)

            @pl.when(s == 0)
            def _():
                slots[n - 1, k] = term[h, at].astype(BF16)

            @pl.when(s > 0)
            def _():
                send(s - 1, d, h).wait_recv()
                slots[s - 1, k] = (term[h, at] + slots[s - 1, k].astype(F32)).astype(BF16)

            @pl.when(s < n - 1)
            def _():
                send(s, d, h).start()

    gradients(0, True)
    for c in inputs(1):
        c.start()
    product(0, me >= 0)

    def step(s, _):
        stream(s, 0)
        product(1, s == 0)

        @pl.when(s < n - 1)
        def _():
            gradients(s + 1, False)

        @pl.when(s < n - 2)
        def _():
            for c in inputs(s + 2):
                c.start()

        stream(s, 1)

        @pl.when(s < n - 1)
        def _():
            product(0, None)

        return 0

    lax.fori_loop(0, n, step, 0)
    for h in range(2):
        for c in results(h):
            c.start()
    for c in d_copies(n - 1):
        c.wait()
    for s in range(n - 1):
        for h in range(2):
            for d in range(2):
                send(s, d, h).wait_send()
    for h in range(2):
        for c in results(h):
            c.wait()


def rs(n, dy, gate, up, wd, wg, wu):
    tokens, width = dy.shape
    ff = gate.shape[1]
    rows = tokens // n
    half, cols = rows // 2, width // 2
    any_ = pl.BlockSpec(memory_space=pl.ANY)
    d = jax.ShapeDtypeStruct((tokens, ff), BF16)
    part = jax.ShapeDtypeStruct((half // 2, width), BF16)
    flops = 2 * tokens * ff * width * 3
    return pl.pallas_call(
        functools.partial(rs_kernel, n),
        name="sum_scatter",
        out_shape=[d, d, d] + [part] * 4,
        in_specs=[any_] * 6,
        out_specs=[any_] * 7,
        scratch_shapes=[
            pltpu.VMEM((ff, width), BF16), pltpu.VMEM((width, ff), BF16), pltpu.VMEM((width, ff), BF16),
            pltpu.VMEM((rows, width), BF16), pltpu.VMEM((rows, ff), BF16), pltpu.VMEM((rows, ff), BF16),
            pltpu.VMEM((rows, ff), BF16), pltpu.VMEM((rows, ff), BF16), pltpu.VMEM((rows, ff), BF16),
            pltpu.VMEM((2, rows, cols), F32),
            pltpu.VMEM((n, 4, half, cols), BF16),
            pltpu.SemaphoreType.DMA((3, 8)), pltpu.SemaphoreType.DMA((2, 3)), pltpu.SemaphoreType.DMA((2, 3)),
            pltpu.SemaphoreType.DMA((n - 1, 4)), pltpu.SemaphoreType.DMA((n - 1, 4)), pltpu.SemaphoreType.DMA((2, 2, 2)),
        ],
        compiler_params=pltpu.CompilerParams(collective_id=0, has_side_effects=True, vmem_limit_bytes=60 * 2**20),
        cost_estimate=pl.CostEstimate(flops=flops, bytes_accessed=60 * 2**20, transcendentals=0),
    )(dy, gate, up, wd, wg, wu)


def place(me, n, k, pair, recv, dx_ref, sem, wait):
    r = recv[0].shape[0]
    for d in range(2):
        chunk = lax.rem(me + n - k, n) if d == 0 else lax.rem(me + k, n)
        at = pl.ds(pl.multiple_of((chunk * 4 + 2 * d + pair) * r, r), r)
        copy = pltpu.make_async_copy(recv[d], dx_ref.at[at], sem.at[d])
        if wait:
            copy.wait()
        else:
            copy.start()


def piece_kernel(n, k, pair, steps, shared, *refs):
    *ins, sem = refs
    n_out = len(shared) + 1 if shared else 1
    outs, ins = ins[-n_out:], ins[:-n_out]
    recv, dx_ref = ins[:2], outs[0]
    me = lax.axis_index("tp")
    i = pl.program_id(0)

    @pl.when(i == 0)
    def _():
        place(me, n, k, pair, recv, dx_ref, sem, False)

    if shared:
        lhs = ins[2]
        for rhs, out in zip(ins[3:3 + len(shared)], outs[1:]):
            out[...] = lax.dot_general(lhs[...], rhs[...], TN, preferred_element_type=F32).astype(BF16)

    @pl.when(i == steps - 1)
    def _():
        place(me, n, k, pair, recv, dx_ref, sem, True)


def piece(n, k, pair, recv, dx, dx_shape, work):
    whole = pl.BlockSpec(recv[0].shape, lambda i: (0, 0))
    hbm = pl.BlockSpec(memory_space=pltpu.HBM)
    operands, in_specs = list(recv), [whole, whole]
    out_shape, out_specs, aliases, carry = [dx_shape], [hbm], {}, ()
    steps, flops, shared = 1, 0, ()
    if work is not None:
        lhs, shared, carry, lhs_spec, rhs_spec, out_spec, steps, shape, flops = work
        operands += [lhs, *shared]
        in_specs += [lhs_spec] + [rhs_spec] * len(shared)
        out_shape += [shape] * len(shared)
        out_specs += [out_spec] * len(shared)
        carry = carry or ()
    if dx is not None:
        aliases[len(operands)] = 0
        operands.append(dx)
        in_specs.append(hbm)
    for i, c in enumerate(carry):
        aliases[len(operands)] = 1 + i
        operands.append(c)
        in_specs.append(pl.BlockSpec(memory_space=pl.ANY))
    out = pl.pallas_call(
        functools.partial(piece_kernel, n, k, pair, steps, shared),
        name="piece",
        grid=(steps,),
        out_shape=out_shape,
        in_specs=in_specs,
        out_specs=out_specs,
        scratch_shapes=[pltpu.SemaphoreType.DMA((2,))],
        input_output_aliases=aliases,
        compiler_params=pltpu.CompilerParams(vmem_limit_bytes=36 * 2**20),
        cost_estimate=pl.CostEstimate(flops=max(flops, 10**8), bytes_accessed=8 * 2**20, transcendentals=0),
    )(*operands)
    return out[0], tuple(out[1:])


def work_in(x, dg, du, carry, j, parts):
    tokens, width = x.shape
    ff = dg.shape[1]
    m, nb = width // parts, 256
    return (x, (dg, du), carry, pl.BlockSpec((tokens, m), lambda i: (0, j)), pl.BlockSpec((tokens, nb), lambda i: (0, i)),
            pl.BlockSpec((m, nb), lambda i: (j, i)), ff // nb, jax.ShapeDtypeStruct((width, ff), BF16), 4 * tokens * m * ff)


def work_out(h, dy, carry, j, parts):
    tokens, width = dy.shape
    ff = h.shape[1]
    nb = 256
    steps = width // parts // nb
    return (h, (dy,), carry, pl.BlockSpec((tokens, ff), lambda i: (0, 0)), pl.BlockSpec((tokens, nb), lambda i: (0, j * steps + i)),
            pl.BlockSpec((ff, nb), lambda i: (0, j * steps + i)), steps, jax.ShapeDtypeStruct((ff, width), BF16), 2 * tokens * ff * width // parts)


def solution(mesh):
    n = mesh.shape["tp"]
    right = [(i, (i + 1) % n) for i in range(n)]
    left = [(i, (i - 1) % n) for i in range(n)]

    def step(x, dy, gate, up, w_gate, w_up, w_down):
        dg, du, h, *bufs = rs(n, dy, gate, up, w_down, w_gate, w_up)
        dx_shape = jax.ShapeDtypeStruct(dy.shape, BF16)
        dx = dw = dw_d = None
        todo = [("out", j) for j in range(4)] + [("in", j) for j in range(8)]

        def hop(pair):
            for d, to in ((0, right), (1, left)):
                bufs[2 * d + pair] = lax.ppermute(bufs[2 * d + pair], "tp", to)

        for k in range(n):
            for pair in range(2):
                recv = (bufs[pair], bufs[2 + pair])
                if k < n - 1:
                    hop(pair)
                if not todo:
                    dx, _ = piece(n, k, pair, recv, dx, dx_shape, None)
                else:
                    kind, j = todo.pop(0)
                    if kind == "in":
                        dx, dw = piece(n, k, pair, recv, dx, dx_shape, work_in(x, dg, du, dw, j, 8))
                    else:
                        dx, dw_d = piece(n, k, pair, recv, dx, dx_shape, work_out(h, dy, dw_d, j, 4))
        return dx, *dw, *dw_d

    tokens, columns, rows = P("dp", None), P(None, "tp"), P("tp", None)
    return jax.shard_map(
        step,
        mesh=mesh,
        in_specs=(tokens, tokens, P("dp", "tp"), P("dp", "tp"), columns, columns, rows),
        out_specs=(tokens, P("dp", "tp"), P("dp", "tp"), P(("dp", "tp"), None)),
        check_vma=False,
    )
```

time: 360 us -> 288 us (0.80)
  the two profiles are of different devices: /device:TPU:21 before, /device:TPU:30 now
where the time goes in v1:
time: 288 us
  Pallas kernels  223 us (77%)
  starting transfers between devices  41 us (14%)
  waiting for transfers between devices  12.2 us (4%)
  local copies, waits for them, and re-layouts  10.8 us (4%)
    pallas_call x1, Pallas kernels, rs(): pl.pallas_call(functools.partial(rs_kernel, n), name='sum_scatter', out_s...  140 us
    pallas_call x16, Pallas kernels, piece(): pl.pallas_call(functools.partial(piece_kernel, n, k, pair, steps, shared)...  82.8 us
    ppermute x28, starting transfers between devices, hop(): bufs[2 * d + pair] = lax.ppermute(bufs[2 * d + pair], 'tp', to)  41 us
    ppermute x28, waiting for transfers between devices, hop(): bufs[2 * d + pair] = lax.ppermute(bufs[2 * d + pair], 'tp', to)  12.2 us
    unnamed x24, local copies, waits for them, and re-layouts  10.8 us
  transfers between devices with their start and end apart: 28, of which 2 were waited for; matrix products, arithmetic and copies ran while one was open for 0% of the time, Pallas kernels for 28%

profile of v1, /device:TPU:30, one launch (start us, length us, event | category | flops | bytes accessed | tf_op | source)
XLA Modules:
  0.0 287.6 jit_solution(10141242577334156461)
XLA Ops:
  0.6 139.8 %sum_scatter.1 = (bf16[2048,1024]{1,0:T(8,128)(2,1)}, bf16[2048,1024]{1,0:T(8,128)(2,1)}, bf16[2048,1024]{1,0:T(8,128)(2,1)}, bf16[64,3072]{1,0:T(8,128)(2,1)}, ...) custom-call(bf16[2048,3072]{1,0:T(8,128)(2,1)} %refs_3_.7, bf16[2048,1024]{1,0:T(8,128)(2,1)} %gate.1, ...), custom_call_target="tpu_custom_call" | custom-call | flops 38654705664 | bytes 62914560 | tf_op jit(solution)/shard_map/sum_scatter/pallas_call | solution.py:197
  140.6 3.2 %collective-permute-start.21 = (bf16[64,3072]{1,0:T(8,128)(2,1)}, bf16[64,3072]{1,0:T(8,128)(2,1)S(1)}, u32[]{:S(2)}, u32[]{:S(2)}) collective-permute-start(bf16[64,3072]{1,0:T(8,128)(2,1)} %get-tuple-element.46.refs_1_), channel_id=1, source_target_pairs={{0,7},{1,0},{2,1},{3,2},{4,3},{5,4},{6,5},{7,6},{8,15},{9,8},{10,9... | collective-permute-start | bytes 1179656 | tf_op jit(solution)/shard_map/ppermute | solution.py:317
  143.8 3.2 %collective-permute-start.7 = (bf16[64,3072]{1,0:T(8,128)(2,1)}, bf16[64,3072]{1,0:T(8,128)(2,1)S(1)}, u32[]{:S(2)}, u32[]{:S(2)}) collective-permute-start(bf16[64,3072]{1,0:T(8,128)(2,1)} %get-tuple-element.44.refs_1_), channel_id=1, source_target_pairs={{0,7},{1,0},{2,1},{3,2},{4,3},{5,4},{6,5},{7,6},{8,15},{9,8},{10,9... | collective-permute-start | bytes 1179656 | tf_op jit(solution)/shard_map/ppermute | solution.py:317
  147.0 6.9 %collective-permute-done.14.refs_0_ = bf16[64,3072]{1,0:T(8,128)(2,1)S(1)} collective-permute-done((bf16[64,3072]{1,0:T(8,128)(2,1)}, bf16[64,3072]{1,0:T(8,128)(2,1)S(1)}, u32[]{:S(2)}, u32[]{:S(2)}) %collective-permute-start.14) | collective-permute-done | bytes 393248 | tf_op jit(solution)/shard_map/ppermute | solution.py:317
  153.9 3.2 %collective-permute-start.22 = (bf16[64,3072]{1,0:T(8,128)(2,1)S(1)}, bf16[64,3072]{1,0:T(8,128)(2,1)S(1)}, u32[]{:S(2)}, u32[]{:S(2)}) collective-permute-start(bf16[64,3072]{1,0:T(8,128)(2,1)S(1)} %collective-permute-done.21.refs_1_), channel_id=1, source_target_pairs={{0,7},{1,0},{2,1},{3,2},{4,3},{5,4},{6,5},{7,6},{8,15},{9,8},{10,9... | collective-permute-start | bytes 1179656 | tf_op jit(solution)/shard_map/ppermute | solution.py:317
  157.2 5.2 %collective-permute-done.refs_0_ = bf16[64,3072]{1,0:T(8,128)(2,1)S(1)} collective-permute-done((bf16[64,3072]{1,0:T(8,128)(2,1)}, bf16[64,3072]{1,0:T(8,128)(2,1)S(1)}, u32[]{:S(2)}, u32[]{:S(2)}) %collective-permute-start) | collective-permute-done | bytes 393248 | tf_op jit(solution)/shard_map/ppermute | solution.py:317
  162.4 3.2 %collective-permute-start.8 = (bf16[64,3072]{1,0:T(8,128)(2,1)S(1)}, bf16[64,3072]{1,0:T(8,128)(2,1)S(1)}, u32[]{:S(2)}, u32[]{:S(2)}) collective-permute-start(bf16[64,3072]{1,0:T(8,128)(2,1)S(1)} %collective-permute-done.7.refs_1_), channel_id=1, source_target_pairs={{0,7},{1,0},{2,1},{3,2},{4,3},{5,4},{6,5},{7,6},{8,15},{9,8},{10,9... | collective-permute-start | bytes 1179656 | tf_op jit(solution)/shard_map/ppermute | solution.py:317
  165.6 4.6 %copy-done.2 = bf16[2048,3072]{1,0:T(8,128)(2,1)S(1)} copy-done((bf16[2048,3072]{1,0:T(8,128)(2,1)S(1)}, bf16[2048,3072]{1,0:T(8,128)(2,1)}, u32[]{:S(2)}) %copy-start.2) | copy-done | bytes 12582936
  174.4 5.3 %piece.16 = (bf16[2048,3072]{1,0:T(8,128)(2,1)}, bf16[1024,3072]{1,0:T(8,128)(2,1)}) custom-call(bf16[64,3072]{1,0:T(8,128)(2,1)S(1)} %copy-done.10, bf16[64,3072]{1,0:T(8,128)(2,1)S(1)} %copy-done.11, bf16[2048,1024]{1,0:T(8,128)(2,1)S(1)} %copy-done.3, bf16[2048,3072]{1,0:T(8,128)(2,1)S(1)} %copy-done.2), custom_call_target="tpu_custom_call" | custom-call | flops 3221225472 | bytes 8388608 | tf_op jit(solution)/shard_map/piece/pallas_call | solution.py:272
  179.7 5.3 %piece.17 = (bf16[2048,3072]{1,0:T(8,128)(2,1)}, bf16[1024,3072]{1,0:T(8,128)(2,1)}) custom-call(bf16[64,3072]{1,0:T(8,128)(2,1)S(1)} %copy-done.8, bf16[64,3072]{1,0:T(8,128)(2,1)S(1)} %copy-done.9, bf16[2048,1024]{1,0:T(8,128)(2,1)S(1)} %copy-done.3, bf16[2048,3072]{1,0:T(8,128)(2,1)S(1)} %copy-done.2, ...), custom_call_target="tpu_custom_call", output_to_operand_aliasing={{0}: (4, {}), {1}: (5, {})} | custom-call | flops 3221225472 | bytes 8388608 | tf_op jit(solution)/shard_map/piece/pallas_call | solution.py:272
  185.2 3.2 %collective-permute-start.23 = (bf16[64,3072]{1,0:T(8,128)(2,1)S(1)}, bf16[64,3072]{1,0:T(8,128)(2,1)S(1)}, u32[]{:S(2)}, u32[]{:S(2)}) collective-permute-start(bf16[64,3072]{1,0:T(8,128)(2,1)S(1)} %collective-permute-done.22.refs_1_), channel_id=1, source_target_pairs={{0,7},{1,0},{2,1},{3,2},{4,3},{5,4},{6,5},{7,6},{8,15},{9,8},{10,9... | collective-permute-start | bytes 1179656 | tf_op jit(solution)/shard_map/ppermute | solution.py:317
  188.4 3.2 %collective-permute-start.9 = (bf16[64,3072]{1,0:T(8,128)(2,1)S(1)}, bf16[64,3072]{1,0:T(8,128)(2,1)S(1)}, u32[]{:S(2)}, u32[]{:S(2)}) collective-permute-start(bf16[64,3072]{1,0:T(8,128)(2,1)S(1)} %collective-permute-done.8.refs_1_), channel_id=1, source_target_pairs={{0,7},{1,0},{2,1},{3,2},{4,3},{5,4},{6,5},{7,6},{8,15},{9,8},{10,9... | collective-permute-start | bytes 1179656 | tf_op jit(solution)/shard_map/ppermute | solution.py:317
  191.7 5.3 %piece.18 = (bf16[2048,3072]{1,0:T(8,128)(2,1)}, bf16[1024,3072]{1,0:T(8,128)(2,1)}) custom-call(bf16[64,3072]{1,0:T(8,128)(2,1)S(1)} %collective-permute-done.14.refs_0_, bf16[64,3072]{1,0:T(8,128)(2,1)S(1)} %collective-permute-done.21.refs_1_, bf16[2048,1024]{1,0:T(8,128)(2,1)S(1)} %copy-done.3, ...), custom_call_target="tpu_custom_call", output_to_operand_aliasing={{0}: (4, {}), {1}: (5, {})} | custom-call | flops 3221225472 | bytes 8388608 | tf_op jit(solution)/shard_map/piece/pallas_call | solution.py:272
  199.0 5.3 %piece.19 = (bf16[2048,3072]{1,0:T(8,128)(2,1)}, bf16[1024,3072]{1,0:T(8,128)(2,1)}) custom-call(bf16[64,3072]{1,0:T(8,128)(2,1)S(1)} %copy-done.5, bf16[64,3072]{1,0:T(8,128)(2,1)S(1)} %copy-done.7, bf16[2048,1024]{1,0:T(8,128)(2,1)S(1)} %copy-done.3, bf16[2048,3072]{1,0:T(8,128)(2,1)S(1)} %copy-done.2, ...), custom_call_target="tpu_custom_call", output_to_operand_aliasing={{0}: (4, {}), {1}: (5, {})} | custom-call | flops 3221225472 | bytes 8388608 | tf_op jit(solution)/shard_map/piece/pallas_call | solution.py:272
  204.4 3.2 %collective-permute-start.24 = (bf16[64,3072]{1,0:T(8,128)(2,1)S(1)}, bf16[64,3072]{1,0:T(8,128)(2,1)S(1)}, u32[]{:S(2)}, u32[]{:S(2)}) collective-permute-start(bf16[64,3072]{1,0:T(8,128)(2,1)S(1)} %collective-permute-done.23.refs_1_), channel_id=1, source_target_pairs={{0,7},{1,0},{2,1},{3,2},{4,3},{5,4},{6,5},{7,6},{8,15},{9,8},{10,9... | collective-permute-start | bytes 1179656 | tf_op jit(solution)/shard_map/ppermute | solution.py:317
  209.7 7.2 %piece.20 = (bf16[2048,3072]{1,0:T(8,128)(2,1)}, bf16[3072,1024]{1,0:T(8,128)(2,1)}, bf16[3072,1024]{1,0:T(8,128)(2,1)}) custom-call(bf16[64,3072]{1,0:T(8,128)(2,1)S(1)} %collective-permute-done.15.refs_0_, bf16[64,3072]{1,0:T(8,128)(2,1)S(1)} %collective-permute-done.22.refs_1_, bf16[2048,3072]{1,0:T(8,128)(2,1)} %refs_2_.15, ...), custom_call_target="tpu_custom_call", output_to_operand_aliasing={{0}: (5, {})} | custom-call | flops 3221225472 | bytes 8388608 | tf_op jit(solution)/shard_map/piece/pallas_call | solution.py:272
  216.9 7.2 %piece.21 = (bf16[2048,3072]{1,0:T(8,128)(2,1)}, bf16[3072,1024]{1,0:T(8,128)(2,1)}, bf16[3072,1024]{1,0:T(8,128)(2,1)}) custom-call(bf16[64,3072]{1,0:T(8,128)(2,1)S(1)} %collective-permute-done.1.refs_0_, bf16[64,3072]{1,0:T(8,128)(2,1)S(1)} %collective-permute-done.8.refs_1_, ...), custom_call_target="tpu_custom_call", output_to_operand_aliasing={{0}: (5, {}), {1}: (6, {}), {2}: (7, {})} | custom-call | flops 3221225472 | bytes 8388608 | tf_op jit(solution)/shard_map/piece/pallas_call | solution.py:272
  224.3 3.2 %collective-permute-start.25 = (bf16[64,3072]{1,0:T(8,128)(2,1)S(1)}, bf16[64,3072]{1,0:T(8,128)(2,1)S(1)}, u32[]{:S(2)}, u32[]{:S(2)}) collective-permute-start(bf16[64,3072]{1,0:T(8,128)(2,1)S(1)} %collective-permute-done.24.refs_1_), channel_id=1, source_target_pairs={{0,7},{1,0},{2,1},{3,2},{4,3},{5,4},{6,5},{7,6},{8,15},{9,8},{10,9... | collective-permute-start | bytes 1179656 | tf_op jit(solution)/shard_map/ppermute | solution.py:317
  229.5 7.2 %piece.22 = (bf16[2048,3072]{1,0:T(8,128)(2,1)}, bf16[3072,1024]{1,0:T(8,128)(2,1)}, bf16[3072,1024]{1,0:T(8,128)(2,1)}) custom-call(bf16[64,3072]{1,0:T(8,128)(2,1)S(1)} %collective-permute-done.16.refs_0_, bf16[64,3072]{1,0:T(8,128)(2,1)S(1)} %collective-permute-done.23.refs_1_, ...), custom_call_target="tpu_custom_call", output_to_operand_aliasing={{0}: (5, {}), {1}: (6, {}), {2}: (7, {})} | custom-call | flops 3221225472 | bytes 8388608 | tf_op jit(solution)/shard_map/piece/pallas_call | solution.py:272
  236.8 7.2 %piece.23 = (bf16[2048,3072]{1,0:T(8,128)(2,1)}, bf16[3072,1024]{1,0:T(8,128)(2,1)}, bf16[3072,1024]{1,0:T(8,128)(2,1)}) custom-call(bf16[64,3072]{1,0:T(8,128)(2,1)S(1)} %collective-permute-done.2.refs_0_, bf16[64,3072]{1,0:T(8,128)(2,1)S(1)} %collective-permute-done.9.refs_1_, ...), custom_call_target="tpu_custom_call", output_to_operand_aliasing={{0}: (5, {}), {1}: (6, {}), {2}: (7, {})} | custom-call | flops 3221225472 | bytes 8388608 | tf_op jit(solution)/shard_map/piece/pallas_call | solution.py:272
  249.4 7.2 %piece.24 = (bf16[2048,3072]{1,0:T(8,128)(2,1)}, bf16[3072,1024]{1,0:T(8,128)(2,1)}, bf16[3072,1024]{1,0:T(8,128)(2,1)}) custom-call(bf16[64,3072]{1,0:T(8,128)(2,1)S(1)} %collective-permute-done.17.refs_0_, bf16[64,3072]{1,0:T(8,128)(2,1)S(1)} %collective-permute-done.24.refs_1_, ...), custom_call_target="tpu_custom_call", output_to_operand_aliasing={{0}: (5, {}), {1}: (6, {}), {2}: (7, {})} | custom-call | flops 3221225472 | bytes 8388608 | tf_op jit(solution)/shard_map/piece/pallas_call | solution.py:272
  256.6 7.2 %piece.25 = (bf16[2048,3072]{1,0:T(8,128)(2,1)}, bf16[3072,1024]{1,0:T(8,128)(2,1)}, bf16[3072,1024]{1,0:T(8,128)(2,1)}) custom-call(bf16[64,3072]{1,0:T(8,128)(2,1)S(1)} %collective-permute-done.3.refs_0_, bf16[64,3072]{1,0:T(8,128)(2,1)S(1)} %collective-permute-done.10.refs_1_, ...), custom_call_target="tpu_custom_call", output_to_operand_aliasing={{0}: (5, {}), {1}: (6, {}), {2}: (7, {})} | custom-call | flops 3221225472 | bytes 8388608 | tf_op jit(solution)/shard_map/piece/pallas_call | solution.py:272
  269.3 7.2 %piece.26 = (bf16[2048,3072]{1,0:T(8,128)(2,1)}, bf16[3072,1024]{1,0:T(8,128)(2,1)}, bf16[3072,1024]{1,0:T(8,128)(2,1)}) custom-call(bf16[64,3072]{1,0:T(8,128)(2,1)S(1)} %collective-permute-done.18.refs_0_, bf16[64,3072]{1,0:T(8,128)(2,1)S(1)} %collective-permute-done.25.refs_1_, ...), custom_call_target="tpu_custom_call", output_to_operand_aliasing={{0}: (5, {}), {1}: (6, {}), {2}: (7, {})} | custom-call | flops 3221225472 | bytes 8388608 | tf_op jit(solution)/shard_map/piece/pallas_call | solution.py:272
  276.5 7.2 %piece.27 = (bf16[2048,3072]{1,0:T(8,128)(2,1)}, bf16[3072,1024]{1,0:T(8,128)(2,1)}, bf16[3072,1024]{1,0:T(8,128)(2,1)}) custom-call(bf16[64,3072]{1,0:T(8,128)(2,1)S(1)} %collective-permute-done.4.refs_0_, bf16[64,3072]{1,0:T(8,128)(2,1)S(1)} %collective-permute-done.11.refs_1_, ...), custom_call_target="tpu_custom_call", output_to_operand_aliasing={{0}: (5, {}), {1}: (6, {}), {2}: (7, {})} | custom-call | flops 3221225472 | bytes 8388608 | tf_op jit(solution)/shard_map/piece/pallas_call | solution.py:272
  (73 shorter events, 25.1 us)
Async XLA Ops:
  153.9 31.1 %collective-permute-start.15 = (bf16[64,3072]{1,0:T(8,128)(2,1)S(1)}, bf16[64,3072]{1,0:T(8,128)(2,1)S(1)}, u32[]{:S(2)}, u32[]{:S(2)}) collective-permute-start(bf16[64,3072]{1,0:T(8,128)(2,1)S(1)} %collective-permute-done.14.refs_0_), channel_id=1, source_target_pairs={{0,1},{1,2},{2,3},{3,4},{4,5},{5,6},{6,7},{7,0},{8,9},{9,10},{10,1... | collective-permute-start | bytes 1179656 | tf_op jit(solution)/shard_map/ppermute | solution.py:317
  153.9 31.2 %collective-permute-start.22 = (bf16[64,3072]{1,0:T(8,128)(2,1)S(1)}, bf16[64,3072]{1,0:T(8,128)(2,1)S(1)}, u32[]{:S(2)}, u32[]{:S(2)}) collective-permute-start(bf16[64,3072]{1,0:T(8,128)(2,1)S(1)} %collective-permute-done.21.refs_1_), channel_id=1, source_target_pairs={{0,7},{1,0},{2,1},{3,2},{4,3},{5,4},{6,5},{7,6},{8,15},{9,8},{10,9... | collective-permute-start | bytes 1179656 | tf_op jit(solution)/shard_map/ppermute | solution.py:317
  162.4 26.0 %collective-permute-start.1 = (bf16[64,3072]{1,0:T(8,128)(2,1)S(1)}, bf16[64,3072]{1,0:T(8,128)(2,1)S(1)}, u32[]{:S(2)}, u32[]{:S(2)}) collective-permute-start(bf16[64,3072]{1,0:T(8,128)(2,1)S(1)} %collective-permute-done.refs_0_), channel_id=1, source_target_pairs={{0,1},{1,2},{2,3},{3,4},{4,5},{5,6},{6,7},{7,0},{8,9},{9,10},{10,1... | collective-permute-start | bytes 1179656 | tf_op jit(solution)/shard_map/ppermute | solution.py:317
  162.4 26.0 %collective-permute-start.8 = (bf16[64,3072]{1,0:T(8,128)(2,1)S(1)}, bf16[64,3072]{1,0:T(8,128)(2,1)S(1)}, u32[]{:S(2)}, u32[]{:S(2)}) collective-permute-start(bf16[64,3072]{1,0:T(8,128)(2,1)S(1)} %collective-permute-done.7.refs_1_), channel_id=1, source_target_pairs={{0,7},{1,0},{2,1},{3,2},{4,3},{5,4},{6,5},{7,6},{8,15},{9,8},{10,9... | collective-permute-start | bytes 1179656 | tf_op jit(solution)/shard_map/ppermute | solution.py:317
  185.1 19.2 %collective-permute-start.16 = (bf16[64,3072]{1,0:T(8,128)(2,1)S(1)}, bf16[64,3072]{1,0:T(8,128)(2,1)S(1)}, u32[]{:S(2)}, u32[]{:S(2)}) collective-permute-start(bf16[64,3072]{1,0:T(8,128)(2,1)S(1)} %collective-permute-done.15.refs_0_), channel_id=1, source_target_pairs={{0,1},{1,2},{2,3},{3,4},{4,5},{5,6},{6,7},{7,0},{8,9},{9,10},{10,1... | collective-permute-start | bytes 1179656 | tf_op jit(solution)/shard_map/ppermute | solution.py:317
  185.2 19.2 %collective-permute-start.23 = (bf16[64,3072]{1,0:T(8,128)(2,1)S(1)}, bf16[64,3072]{1,0:T(8,128)(2,1)S(1)}, u32[]{:S(2)}, u32[]{:S(2)}) collective-permute-start(bf16[64,3072]{1,0:T(8,128)(2,1)S(1)} %collective-permute-done.22.refs_1_), channel_id=1, source_target_pairs={{0,7},{1,0},{2,1},{3,2},{4,3},{5,4},{6,5},{7,6},{8,15},{9,8},{10,9... | collective-permute-start | bytes 1179656 | tf_op jit(solution)/shard_map/ppermute | solution.py:317
  188.4 19.3 %collective-permute-start.2 = (bf16[64,3072]{1,0:T(8,128)(2,1)S(1)}, bf16[64,3072]{1,0:T(8,128)(2,1)S(1)}, u32[]{:S(2)}, u32[]{:S(2)}) collective-permute-start(bf16[64,3072]{1,0:T(8,128)(2,1)S(1)} %collective-permute-done.1.refs_0_), channel_id=1, source_target_pairs={{0,1},{1,2},{2,3},{3,4},{4,5},{5,6},{6,7},{7,0},{8,9},{9,10},{10,1... | collective-permute-start | bytes 1179656 | tf_op jit(solution)/shard_map/ppermute | solution.py:317
  188.4 19.2 %collective-permute-start.9 = (bf16[64,3072]{1,0:T(8,128)(2,1)S(1)}, bf16[64,3072]{1,0:T(8,128)(2,1)S(1)}, u32[]{:S(2)}, u32[]{:S(2)}) collective-permute-start(bf16[64,3072]{1,0:T(8,128)(2,1)S(1)} %collective-permute-done.8.refs_1_), channel_id=1, source_target_pairs={{0,7},{1,0},{2,1},{3,2},{4,3},{5,4},{6,5},{7,6},{8,15},{9,8},{10,9... | collective-permute-start | bytes 1179656 | tf_op jit(solution)/shard_map/ppermute | solution.py:317
  204.3 19.9 %collective-permute-start.17 = (bf16[64,3072]{1,0:T(8,128)(2,1)S(1)}, bf16[64,3072]{1,0:T(8,128)(2,1)S(1)}, u32[]{:S(2)}, u32[]{:S(2)}) collective-permute-start(bf16[64,3072]{1,0:T(8,128)(2,1)S(1)} %collective-permute-done.16.refs_0_), channel_id=1, source_target_pairs={{0,1},{1,2},{2,3},{3,4},{4,5},{5,6},{6,7},{7,0},{8,9},{9,10},{10,1... | collective-permute-start | bytes 1179656 | tf_op jit(solution)/shard_map/ppermute | solution.py:317
  204.4 19.9 %collective-permute-start.24 = (bf16[64,3072]{1,0:T(8,128)(2,1)S(1)}, bf16[64,3072]{1,0:T(8,128)(2,1)S(1)}, u32[]{:S(2)}, u32[]{:S(2)}) collective-permute-start(bf16[64,3072]{1,0:T(8,128)(2,1)S(1)} %collective-permute-done.23.refs_1_), channel_id=1, source_target_pairs={{0,7},{1,0},{2,1},{3,2},{4,3},{5,4},{6,5},{7,6},{8,15},{9,8},{10,9... | collective-permute-start | bytes 1179656 | tf_op jit(solution)/shard_map/ppermute | solution.py:317
  207.6 19.9 %collective-permute-start.10 = (bf16[64,3072]{1,0:T(8,128)(2,1)S(1)}, bf16[64,3072]{1,0:T(8,128)(2,1)S(1)}, u32[]{:S(2)}, u32[]{:S(2)}) collective-permute-start(bf16[64,3072]{1,0:T(8,128)(2,1)S(1)} %collective-permute-done.9.refs_1_), channel_id=1, source_target_pairs={{0,7},{1,0},{2,1},{3,2},{4,3},{5,4},{6,5},{7,6},{8,15},{9,8},{10,9... | collective-permute-start | bytes 1179656 | tf_op jit(solution)/shard_map/ppermute | solution.py:317
  207.7 19.9 %collective-permute-start.3 = (bf16[64,3072]{1,0:T(8,128)(2,1)S(1)}, bf16[64,3072]{1,0:T(8,128)(2,1)S(1)}, u32[]{:S(2)}, u32[]{:S(2)}) collective-permute-start(bf16[64,3072]{1,0:T(8,128)(2,1)S(1)} %collective-permute-done.2.refs_0_), channel_id=1, source_target_pairs={{0,1},{1,2},{2,3},{3,4},{4,5},{5,6},{6,7},{7,0},{8,9},{9,10},{10,1... | collective-permute-start | bytes 1179656 | tf_op jit(solution)/shard_map/ppermute | solution.py:317
  224.2 19.9 %collective-permute-start.18 = (bf16[64,3072]{1,0:T(8,128)(2,1)S(1)}, bf16[64,3072]{1,0:T(8,128)(2,1)S(1)}, u32[]{:S(2)}, u32[]{:S(2)}) collective-permute-start(bf16[64,3072]{1,0:T(8,128)(2,1)S(1)} %collective-permute-done.17.refs_0_), channel_id=1, source_target_pairs={{0,1},{1,2},{2,3},{3,4},{4,5},{5,6},{6,7},{7,0},{8,9},{9,10},{10,1... | collective-permute-start | bytes 1179656 | tf_op jit(solution)/shard_map/ppermute | solution.py:317
  224.3 19.9 %collective-permute-start.25 = (bf16[64,3072]{1,0:T(8,128)(2,1)S(1)}, bf16[64,3072]{1,0:T(8,128)(2,1)S(1)}, u32[]{:S(2)}, u32[]{:S(2)}) collective-permute-start(bf16[64,3072]{1,0:T(8,128)(2,1)S(1)} %collective-permute-done.24.refs_1_), channel_id=1, source_target_pairs={{0,7},{1,0},{2,1},{3,2},{4,3},{5,4},{6,5},{7,6},{8,15},{9,8},{10,9... | collective-permute-start | bytes 1179656 | tf_op jit(solution)/shard_map/ppermute | solution.py:317
  227.5 19.9 %collective-permute-start.11 = (bf16[64,3072]{1,0:T(8,128)(2,1)S(1)}, bf16[64,3072]{1,0:T(8,128)(2,1)S(1)}, u32[]{:S(2)}, u32[]{:S(2)}) collective-permute-start(bf16[64,3072]{1,0:T(8,128)(2,1)S(1)} %collective-permute-done.10.refs_1_), channel_id=1, source_target_pairs={{0,7},{1,0},{2,1},{3,2},{4,3},{5,4},{6,5},{7,6},{8,15},{9,8},{10,9... | collective-permute-start | bytes 1179656 | tf_op jit(solution)/shard_map/ppermute | solution.py:317
  227.6 19.9 %collective-permute-start.4 = (bf16[64,3072]{1,0:T(8,128)(2,1)S(1)}, bf16[64,3072]{1,0:T(8,128)(2,1)S(1)}, u32[]{:S(2)}, u32[]{:S(2)}) collective-permute-start(bf16[64,3072]{1,0:T(8,128)(2,1)S(1)} %collective-permute-done.3.refs_0_), channel_id=1, source_target_pairs={{0,1},{1,2},{2,3},{3,4},{4,5},{5,6},{6,7},{7,0},{8,9},{9,10},{10,1... | collective-permute-start | bytes 1179656 | tf_op jit(solution)/shard_map/ppermute | solution.py:317
  244.0 19.9 %collective-permute-start.19 = (bf16[64,3072]{1,0:T(8,128)(2,1)S(1)}, bf16[64,3072]{1,0:T(8,128)(2,1)S(1)}, u32[]{:S(2)}, u32[]{:S(2)}) collective-permute-start(bf16[64,3072]{1,0:T(8,128)(2,1)S(1)} %collective-permute-done.18.refs_0_), channel_id=1, source_target_pairs={{0,1},{1,2},{2,3},{3,4},{4,5},{5,6},{6,7},{7,0},{8,9},{9,10},{10,1... | collective-permute-start | bytes 1179656 | tf_op jit(solution)/shard_map/ppermute | solution.py:317
  244.2 19.9 %collective-permute-start.26 = (bf16[64,3072]{1,0:T(8,128)(2,1)S(1)}, bf16[64,3072]{1,0:T(8,128)(2,1)S(1)}, u32[]{:S(2)}, u32[]{:S(2)}) collective-permute-start(bf16[64,3072]{1,0:T(8,128)(2,1)S(1)} %collective-permute-done.25.refs_1_), channel_id=1, source_target_pairs={{0,7},{1,0},{2,1},{3,2},{4,3},{5,4},{6,5},{7,6},{8,15},{9,8},{10,9... | collective-permute-start | bytes 1179656 | tf_op jit(solution)/shard_map/ppermute | solution.py:317
  247.4 19.9 %collective-permute-start.12 = (bf16[64,3072]{1,0:T(8,128)(2,1)S(1)}, bf16[64,3072]{1,0:T(8,128)(2,1)S(1)}, u32[]{:S(2)}, u32[]{:S(2)}) collective-permute-start(bf16[64,3072]{1,0:T(8,128)(2,1)S(1)} %collective-permute-done.11.refs_1_), channel_id=1, source_target_pairs={{0,7},{1,0},{2,1},{3,2},{4,3},{5,4},{6,5},{7,6},{8,15},{9,8},{10,9... | collective-permute-start | bytes 1179656 | tf_op jit(solution)/shard_map/ppermute | solution.py:317
  247.5 20.1 %collective-permute-start.5 = (bf16[64,3072]{1,0:T(8,128)(2,1)S(1)}, bf16[64,3072]{1,0:T(8,128)(2,1)S(1)}, u32[]{:S(2)}, u32[]{:S(2)}) collective-permute-start(bf16[64,3072]{1,0:T(8,128)(2,1)S(1)} %collective-permute-done.4.refs_0_), channel_id=1, source_target_pairs={{0,1},{1,2},{2,3},{3,4},{4,5},{5,6},{6,7},{7,0},{8,9},{9,10},{10,1... | collective-permute-start | bytes 1179656 | tf_op jit(solution)/shard_map/ppermute | solution.py:317
  263.9 21.7 %collective-permute-start.20 = (bf16[64,3072]{1,0:T(8,128)(2,1)S(1)}, bf16[64,3072]{1,0:T(8,128)(2,1)S(1)}, u32[]{:S(2)}, u32[]{:S(2)}) collective-permute-start(bf16[64,3072]{1,0:T(8,128)(2,1)S(1)} %collective-permute-done.19.refs_0_), channel_id=1, source_target_pairs={{0,1},{1,2},{2,3},{3,4},{4,5},{5,6},{6,7},{7,0},{8,9},{9,10},{10,1... | collective-permute-start | bytes 1179656 | tf_op jit(solution)/shard_map/ppermute | solution.py:317
  264.0 21.6 %collective-permute-start.27 = (bf16[64,3072]{1,0:T(8,128)(2,1)S(1)}, bf16[64,3072]{1,0:T(8,128)(2,1)S(1)}, u32[]{:S(2)}, u32[]{:S(2)}) collective-permute-start(bf16[64,3072]{1,0:T(8,128)(2,1)S(1)} %collective-permute-done.26.refs_1_), channel_id=1, source_target_pairs={{0,7},{1,0},{2,1},{3,2},{4,3},{5,4},{6,5},{7,6},{8,15},{9,8},{10,9... | collective-permute-start | bytes 1179656 | tf_op jit(solution)/shard_map/ppermute | solution.py:317
  267.2 19.3 %collective-permute-start.13 = (bf16[64,3072]{1,0:T(8,128)(2,1)S(1)}, bf16[64,3072]{1,0:T(8,128)(2,1)S(1)}, u32[]{:S(2)}, u32[]{:S(2)}) collective-permute-start(bf16[64,3072]{1,0:T(8,128)(2,1)S(1)} %collective-permute-done.12.refs_1_), channel_id=1, source_target_pairs={{0,7},{1,0},{2,1},{3,2},{4,3},{5,4},{6,5},{7,6},{8,15},{9,8},{10,9... | collective-permute-start | bytes 1179656 | tf_op jit(solution)/shard_map/ppermute | solution.py:317
  267.6 19.0 %collective-permute-start.6 = (bf16[64,3072]{1,0:T(8,128)(2,1)S(1)}, bf16[64,3072]{1,0:T(8,128)(2,1)S(1)}, u32[]{:S(2)}, u32[]{:S(2)}) collective-permute-start(bf16[64,3072]{1,0:T(8,128)(2,1)S(1)} %collective-permute-done.5.refs_0_), channel_id=1, source_target_pairs={{0,1},{1,2},{2,3},{3,4},{4,5},{5,6},{6,7},{7,0},{8,9},{9,10},{10,1... | collective-permute-start | bytes 1179656 | tf_op jit(solution)/shard_map/ppermute | solution.py:317
  (16 other events, 141.6 us)
